TPU v7x, 32 devices: a whole 2x2x4 slice. The times are simulated.
32 devices in a mesh: seq: 8 (over z, x), head: 4 (over y, core).
Axes of the slice: x: 2, y: 2, z: 4, core: 2. Of those that a mesh axis runs over, the one named last changes fastest.
Arguments:
- queries: bfloat16 [8192, 4096], P('seq', 'head'), may hold values from -150 to 150
- keys: bfloat16 [8192, 4096], P('seq', 'head'), may hold values from -7 to 7
- values: bfloat16 [8192, 4096], P('seq', 'head'), may hold values from -6 to 6
- random_holder: int32 [32, 64, 3], P('head', 'seq'), may hold values from 0 to 7, all different within a row; in each aligned block of 8 rows (0 to 7, 8 to 15, ..., all dimensions but the last counted through in order) at most 3 rows name the same one
- random_offset: int32 [32, 64, 3], P('head', 'seq'), may hold values from 0 to 7
- keep: int32 [64], P('seq'), may hold values from 0 to 1, as said below
Outputs:
- packed: bfloat16 [8192, 4096], P('seq', 'head')
Inputs may be any that keep to these rules, and one draw needn't show every extreme that they name: `random_holder`: for each head, the 8 query blocks of one index of seq name no index of seq more than 3 times over all their random entries; the 3 entries of one query block and head differ. `keep`: block j is kept where j % 8 == 0 or j % 8 == 7, and not kept where j % 8 == 1.
All inputs are finite; a program needn't handle non-finite values.
Results may differ from a plain program's by a relative error of at most 0.007.
Values may be sent and summed in bfloat16 or wider, within the bound.
A program may use at most 128 MiB of HBM per device.

v0:
```python
import functools
import math

import jax
import jax.numpy as jnp
from jax import lax
from jax.sharding import PartitionSpec as P

DH = 128
B = 128
G = 2
R = 3


neg_big = -1e30


def extended_2(block, sides, width):
    for axis, dim in sides:
        count = lax.axis_size(axis)
        forward = [(i, i + 1) for i in range(count - 1)]
        backward = [(target, source) for source, target in forward]
        low = lax.ppermute(
            lax.slice_in_dim(block, block.shape[dim] - width, None, axis=dim), axis, forward
        )
        high = lax.ppermute(lax.slice_in_dim(block, 0, width, axis=dim), axis, backward)
        block = jnp.concatenate([low, block, high], axis=dim)
    return block


def broadcast(block, axis, source):
    block = jnp.where(lax.axis_index(axis) == source, block, jnp.zeros_like(block))
    return lax.psum(block, axis)


def prefix(value, axis, join, neutral):
    count, mine = (lax.axis_size(axis), lax.axis_index(axis))
    pieces = lax.all_gather(value, axis)
    subtotal = jnp.full_like(value, 0) + jnp.asarray(neutral, value.dtype)

    def hop(position, subtotal):
        longer = join(subtotal, pieces[position])
        return jnp.where(position < mine, longer, subtotal)

    return lax.fori_loop(0, count - 1, hop, subtotal)


def shifted(x, axis, by):
    size = lax.axis_size(axis)
    pairs = [(i, i + by) for i in range(size) if 0 <= i + by < size]
    return lax.ppermute(x, axis, pairs)


def tile_stats(query_blocks, key_tile, value_tile, spec_scores, spec_out, score_scale):
    scores = (
        jnp.einsum(spec_scores, query_blocks, key_tile, preferred_element_type=jnp.float32)
        * score_scale
    )
    row_max = jnp.max(scores, axis=-1)
    weights = jnp.exp(scores - row_max[..., None]).astype(jnp.bfloat16)
    row_sum = jnp.sum(weights, axis=-1, dtype=jnp.float32)
    summed = jnp.einsum(spec_out, weights, value_tile, preferred_element_type=jnp.float32)
    return (row_max, row_sum, summed)


def merge_tiles(parts):
    peaks = [jnp.where(live, row_max, neg_big) for live, row_max, row_sum, summed in parts]
    overall = functools.reduce(jnp.maximum, peaks)
    numer = jnp.zeros(parts[0][3].shape, jnp.float32)
    denom = jnp.zeros(parts[0][1].shape, jnp.float32)
    for live, row_max, row_sum, summed in parts:
        factor = jnp.where(live, jnp.exp(row_max - overall), 0.0)
        numer = numer + factor[..., None] * summed
        denom = denom + factor * row_sum
    return numer / denom[..., None]


def add_counts(earlier, later):
    return earlier + later


def body(queries, keys, values, random_holder, random_offset, keep):
    tok_dev, width_dev = queries.shape
    blk_dev = tok_dev // B
    head_dev = width_dev // DH
    seq_count = lax.axis_size("seq")
    my_index = lax.axis_index("seq")
    score_scale = 1.0 / math.sqrt(DH)
    query_blocks = queries.reshape(blk_dev, B, head_dev, DH)
    key_value = jnp.stack((keys, values))
    block_ids = my_index * blk_dev + jnp.arange(blk_dev, dtype=jnp.int32)
    extended = extended_2(key_value, (("seq", 1),), B)
    parts = []
    for shift_by in (-1, 0, 1):
        near_tiles = lax.slice_in_dim(
            extended, (1 + shift_by) * B, (1 + shift_by) * B + tok_dev, axis=1
        )
        near_tiles = near_tiles.reshape(2, blk_dev, B, head_dev, DH)
        neighbour = block_ids + shift_by
        live = ((neighbour >= 0) & (neighbour < blk_dev * seq_count))[:, None, None]
        parts.append(
            (live,)
            + tile_stats(
                query_blocks,
                near_tiles[0],
                near_tiles[1],
                "nqhd,nkhd->nqhk",
                "nqhk,nkhd->nqhd",
                score_scale,
            )
        )
    shared = broadcast(key_value[:, : G * B], "seq", 0).reshape(2, G, B, head_dev, DH)
    for glob_pos in range(G):
        parts.append(
            (True,)
            + tile_stats(
                query_blocks,
                shared[0, glob_pos],
                shared[1, glob_pos],
                "nqhd,khd->nqhk",
                "nqhk,khd->nqhd",
                score_scale,
            )
        )
    count_req = blk_dev * R
    capacity = max(2, (count_req + seq_count - 1) // seq_count)
    holders = random_holder.reshape(head_dev, count_req)
    offset_idx = random_offset.reshape(head_dev, count_req)
    onehot = (holders[..., None] == jnp.arange(seq_count, dtype=jnp.int32)).astype(jnp.int32)
    rank = jnp.sum((jnp.cumsum(onehot, axis=1) - onehot) * onehot, axis=-1)
    selector = onehot[..., None] * (
        rank[:, :, None, None] == jnp.arange(capacity, dtype=jnp.int32)
    ).astype(jnp.int32)
    asked_slots = jnp.transpose(
        jnp.sum(selector * (offset_idx + 1)[:, :, None, None], axis=1), (1, 0, 2)
    )
    tiles_kv = key_value.reshape(2, blk_dev, B, head_dev, DH)
    asked = lax.all_to_all(asked_slots, "seq", split_axis=0, concat_axis=0, tiled=True)
    entry = jnp.maximum(asked - 1, 0)
    head_idx = jnp.arange(asked.shape[1], dtype=jnp.int32)[None, :, None]
    picked = tiles_kv[:, entry, :, head_idx, :]
    picked = jnp.where((asked > 0)[..., None, None, None], picked, jnp.zeros_like(picked))
    replies = lax.all_to_all(picked, "seq", split_axis=0, concat_axis=0, tiled=True)
    head_rows = jnp.arange(head_dev, dtype=jnp.int32)[:, None]
    fetched = replies[holders, head_rows, rank].reshape(head_dev, blk_dev, R, 2, B, DH)
    for rand_pos in range(R):
        parts.append(
            (True,)
            + tile_stats(
                query_blocks,
                fetched[:, :, rand_pos, 0],
                fetched[:, :, rand_pos, 1],
                "nqhd,hnkd->nqhk",
                "nqhk,hnkd->nqhd",
                score_scale,
            )
        )
    attended = merge_tiles(parts).astype(jnp.bfloat16).reshape(blk_dev, B * width_dev)
    kept_count = jnp.sum(keep)
    start_rank = prefix(kept_count, "seq", add_counts, jnp.int32(0))
    local_rank = jnp.cumsum(keep) - keep
    target = start_rank + local_rank
    blocks = jnp.where((keep > 0)[:, None], attended, jnp.zeros_like(attended))
    slot = target % blk_dev
    distance = jnp.where(keep > 0, my_index - target // blk_dev, 0)
    placing = (slot[None, :] == jnp.arange(blk_dev, dtype=jnp.int32)[:, None]) & (keep > 0)[None, :]
    blocks = jnp.dot(
        placing.astype(jnp.bfloat16), blocks, preferred_element_type=jnp.float32
    ).astype(jnp.bfloat16)
    distance = jnp.sum(placing.astype(jnp.int32) * distance[None, :], axis=1)
    for bit_pos in range((seq_count - 1).bit_length()):
        stride = 2**bit_pos
        moving = distance // stride % 2 > 0
        moved = jnp.where(moving[:, None], blocks, jnp.zeros_like(blocks))
        moved_dist = jnp.where(moving, distance, 0).astype(jnp.bfloat16)
        staying = jnp.where(moving[:, None], jnp.zeros_like(blocks), blocks)
        staying_dist = jnp.where(moving, 0, distance)
        arrived, arrived_dist = shifted((moved, moved_dist), "seq", -stride)
        blocks = staying + arrived
        distance = staying_dist + arrived_dist.astype(jnp.int32)
    return blocks.reshape(tok_dev, width_dev)


def solution(mesh):
    in_specs = (
        P("seq", "head"),
        P("seq", "head"),
        P("seq", "head"),
        P("head", "seq", None),
        P("head", "seq", None),
        P("seq"),
    )
    out_specs = P("seq", "head")
    return jax.shard_map(body, mesh=mesh, in_specs=in_specs, out_specs=out_specs, check_vma=False)
```

profile of v0, /device:TPU:2, one launch (start us, length us, event | category | flops | bytes accessed | tf_op | source)
XLA Modules:
  0.0 687.2 jit_solution(10262043809626712274)
XLA Ops:
  10.3 6.3 all-to-all-start
  25.6 11.3 %gather_fusion = bf16[192,2,128,128]{3,2,1,0:T(8,128)(2,1)} fusion(bf16[2,8,128,8,128]{4,2,3,1,0:T(8,128)(2,1)} %pad_maximum_fusion, s32[192]{0:T(256)S(1)} %reshape.395), kind=kCustom, calls=%fused_computation | custom fusion | bytes 25167360 | tf_op jit(solution)/shard_map/gather | solution.py:141
  37.0 10.7 %broadcast_select_fusion = bf16[8,8,3,2,128,128]{5,4,3,2,1,0:T(8,128)(2,1)} fusion(bf16[8,8,3,2,128,128]{5,4,3,2,1,0:T(8,128)(2,1)} %bitcast.270, pred[8,8,3]{2,1,0:T(8,128)(4,1)S(1)} %copy.301), kind=kLoop, calls=%fused_computation.3 | loop fusion | flops 6291456 | bytes 25166016 | tf_op jit(solution)/shard_map/jit(_where)/select_n | solution.py:142
  47.7 6.0 all-to-all-start.1
  55.6 3.4 collective-permute-start.2
  67.9 280.5 %all-reduce = s32[8]{0:T(128)S(1)} all-reduce(s32[8]{0:T(128)S(1)} %dynamic-update-slice), channel_id=1, replica_groups=mesh['seq'=8,'head'=4] {'seq'}, use_global_device_ids=true, to_apply=%add | all-reduce | flops 8 | bytes 64
  350.8 9.4 %while.13 = (s32[]{:T(128)}, s32[]{:T(128)}, s32[]{:T(128)}, s32[8]{0:T(128)S(1)}, s32[]{:T(128)}) while((s32[]{:T(128)}, s32[]{:T(128)}, s32[]{:T(128)}, s32[8]{0:T(128)S(1)}, s32[]{:T(128)}) %tuple.68), condition=%wide.region_2.0_spmd, body=%wide.region_1.0_spmd.sunk | while | flops 5 | bytes 107 | solution.py:45
  362.0 5.1 bitcast_reduce_fusion.6
  367.8 6.2 fusion.42
  374.0 5.6 maximum_bitcast_fusion.1
  388.5 3.3 fusion.44
  405.0 14.2 %gather_fusion.1 = bf16[192,2,128,128]{3,2,1,0:T(8,128)(2,1)} fusion(bf16[8,8,3,2,128,128]{5,4,3,2,1,0:T(8,128)(2,1)} %all-to-all-done.1, s32[192]{0:T(256)S(1)} %reshape.401), kind=kCustom, calls=%fused_computation.1 | custom fusion | bytes 25168128 | tf_op jit(solution)/shard_map/gather | solution.py:145
  419.2 7.9 %fusion.108 = (bf16[8,8,1,1,128,128]{5,4,3,2,1,0:T(8,128)(2,1)S(1)}, bf16[8,8,1,1,128,128]{5,4,3,2,1,0:T(8,128)(2,1)}, bf16[8,8,1,1,128,128]{5,4,3,2,1,0:T(8,128...) fusion(bf16[8,8,3,2,128,128]{5,4,3,2,1,0:T(8,128)(2,1)} %bitcas, ...), kind=kLoop, calls=%fused_computation.210 | loop fusion | bytes 25165824 | tf_op jit(solution)/shard_map/slice | solution.py:151
  427.1 3.6 bitcast_reduce_fusion.1
  430.6 3.6 bitcast_reduce_fusion
  434.2 3.5 bitcast_reduce_fusion.2
  437.7 4.0 copy.356
  441.7 6.4 convert_reduce_fusion.2
  456.8 5.8 fusion.32
  466.5 12.7 %fusion.2 = bf16[8,128,8,128]{1,3,2,0:T(8,128)(2,1)} fusion(f32[8,8,128,128]{3,2,1,0:T(8,128)} %fusion.32, f32[8,8,128,128]{3,2,1,0:T(8,128)} %fusion.34, f32[8,128,8,128]{3,1,0,2:T(8,128)} %fusion.36, f32[8,128,8,128]{3,1,0,2:T(8,128)} %fusion.38, f32[8,8,128,128]{3,2,1,0:T(8,128)} %fusion.40, f32[8,8,128,128]{2,3,1,0:T(8,128)} %fusion.42, ...), kind=kOutput, calls=%fused_computation.8 | convolution fusion | flops 289406976 | bytes 38076416 | tf_op jit(solution)/shard_map/nqhk,hnkd->nqhd/dot_general | solution.py:62
  483.9 7.2 %collective-permute-start.4 = (bf16[8,131072]{1,0:T(8,128)(2,1)S(1)}, bf16[8,131072]{1,0:T(8,128)(2,1)S(1)}, u32[]{:S(2)}, u32[]{:S(2)}) collective-permute-start(bf16[8,131072]{1,0:T(8,128)(2,1)S(1)} %get-tuple-element.145), channel_id=1, source_target_pairs={{4,0},{8,4},{12,8},{16,12},{20,16},{24,20},{28,24},{5,1},{9,5},{13... | collective-permute-start | bytes 6291464 | tf_op jit(solution)/shard_map/ppermute | solution.py:51
  493.1 40.4 %collective-permute-done = bf16[8]{0:T(256)(128)(2,1)S(1)} collective-permute-done((bf16[8]{0:T(256)(128)(2,1)S(1)}, bf16[8]{0:T(256)(128)(2,1)S(1)}, u32[]{:S(2)}, u32[]{:S(2)}) %collective-permute-start) | collective-permute-done | bytes 48 | tf_op jit(solution)/shard_map/ppermute | solution.py:51
  536.4 47.1 %collective-permute-done.1 = bf16[8]{0:T(256)(128)(2,1)S(1)} collective-permute-done((bf16[8]{0:T(256)(128)(2,1)S(1)}, bf16[8]{0:T(256)(128)(2,1)S(1)}, u32[]{:S(2)}, u32[]{:S(2)}) %collective-permute-start.1) | collective-permute-done | bytes 48 | tf_op jit(solution)/shard_map/ppermute | solution.py:51
  585.3 92.0 %collective-permute-done.6 = bf16[8,131072]{1,0:T(8,128)(2,1)S(1)} collective-permute-done((bf16[8,131072]{1,0:T(8,128)(2,1)S(1)}, bf16[8,131072]{1,0:T(8,128)(2,1)S(1)}, u32[]{:S(2)}, u32[]{:S(2)}) %collective-permute-start.6) | collective-permute-done | bytes 2097184 | tf_op jit(solution)/shard_map/ppermute | solution.py:51
  (138 shorter events, 81.2 us)
Async XLA Ops:
  10.3 15.0 %all-to-all-start = ((s32[8,8,3]{1,2,0:T(4,128)}), s32[8,8,3]{1,2,0:T(4,128)S(1)}, u32[]{:S(2)}, u32[]{:S(2)}) async-start(s32[8,8,3]{1,2,0:T(4,128)} %copy.299), calls=%async_computation | async-start | bytes 32768 | tf_op jit(solution)/shard_map/all_to_all | solution.py:138
  16.6 3.8 copy-start.5
  47.7 357.3 %all-to-all-start.1 = ((bf16[8,8,3,2,128,128]{5,4,3,2,1,0:T(8,128)(2,1)}), bf16[8,8,3,2,128,128]{5,4,3,2,1,0:T(8,128)(2,1)}, u32[]{:S(2)}, u32[]{:S(2)}) async-start(bf16[8,8,3,2,128,128]{5,4,3,2,1,0:T(8,128)(2,1)} %broadcast_select_fusion), calls=%async_computation.1 | async-start | bytes 25165824 | tf_op jit(solution)/shard_map/all_to_all | solution.py:143
  53.7 340.7 %all-reduce.3.cloned.1.call-start = ((), (), s32[]{:S(2)}) async-start(), calls=%async_computation.2 | async-start | bytes 2097152 | tf_op jit(solution)/shard_map/psum | solution.py:33
  55.6 318.4 %collective-permute-start.2 = (bf16[2,128,1024]{2,1,0:T(8,128)(2,1)}, bf16[2,128,1024]{2,1,0:T(8,128)(2,1)}, u32[]{:S(2)}, u32[]{:S(2)}) collective-permute-start(bf16[2,128,1024]{2,1,0:T(8,128)(2,1)} %get-tuple-element.125), channel_id=1, source_target_pairs={{0,4},{4,8},{8,12},{12,16},{16,20},{20,24},{24,28},{1,5},{5,9},{9,... | collective-permute-start | bytes 1572872 | tf_op jit(solution)/shard_map/ppermute | solution.py:23
  59.0 315.0 %collective-permute-start.3 = (bf16[2,128,1024]{2,1,0:T(8,128)(2,1)S(1)}, bf16[2,128,1024]{2,1,0:T(8,128)(2,1)}, u32[]{:S(2)}, u32[]{:S(2)}) collective-permute-start(bf16[2,128,1024]{2,1,0:T(8,128)(2,1)S(1)} %get-tuple-element.126), channel_id=1, source_target_pairs={{4,0},{8,4},{12,8},{16,12},{20,16},{24,20},{28,24},{5,1},{9,5},{13... | collective-permute-start | bytes 1572872 | tf_op jit(solution)/shard_map/ppermute | solution.py:26
  62.3 3.5 copy-start.23
  360.8 6.2 copy-start.14
  367.7 6.3 copy-start.6
  367.8 6.3 copy-start.7
  383.1 3.2 copy-start.1
  388.5 3.3 copy-start.2
  441.7 6.4 copy-start.4
  441.7 6.4 copy-start.11
  456.8 5.8 copy-start
  456.8 6.4 copy-start.3
  479.2 3.3 copy-start.15
  479.2 3.3 copy-start.18
  482.4 8.7 %copy-start.22 = (bf16[8]{0:T(256)(128)(2,1)S(1)}, bf16[8]{0:T(256)(128)(2,1)}, u32[]{:S(2)}) copy-start(bf16[8]{0:T(256)(128)(2,1)} %get-tuple-element.111) | copy-start | bytes 52
  483.9 49.6 %collective-permute-start.4 = (bf16[8,131072]{1,0:T(8,128)(2,1)S(1)}, bf16[8,131072]{1,0:T(8,128)(2,1)S(1)}, u32[]{:S(2)}, u32[]{:S(2)}) collective-permute-start(bf16[8,131072]{1,0:T(8,128)(2,1)S(1)} %get-tuple-element.145), channel_id=1, source_target_pairs={{4,0},{8,4},{12,8},{16,12},{20,16},{24,20},{28,24},{5,1},{9,5},{13... | collective-permute-start | bytes 6291464 | tf_op jit(solution)/shard_map/ppermute | solution.py:51
  491.2 42.3 %collective-permute-start = (bf16[8]{0:T(256)(128)(2,1)S(1)}, bf16[8]{0:T(256)(128)(2,1)S(1)}, u32[]{:S(2)}, u32[]{:S(2)}) collective-permute-start(bf16[8]{0:T(256)(128)(2,1)S(1)} %copy-done.22), channel_id=1, source_target_pairs={{4,0},{8,4},{12,8},{16,12},{20,16},{24,20},{28,24},{5,1},{9,5},{13... | collective-permute-start | bytes 56 | tf_op jit(solution)/shard_map/ppermute | solution.py:51
  533.8 49.7 %collective-permute-start.5 = (bf16[8,131072]{1,0:T(8,128)(2,1)S(1)}, bf16[8,131072]{1,0:T(8,128)(2,1)S(1)}, u32[]{:S(2)}, u32[]{:S(2)}) collective-permute-start(bf16[8,131072]{1,0:T(8,128)(2,1)S(1)} %broadcast_select_fusion.2), channel_id=1, source_target_pairs={{8,0},{12,4},{16,8},{20,12},{24,16},{28,20},{9,1},{13,5},{17,9},{2... | collective-permute-start | bytes 6291464 | tf_op jit(solution)/shard_map/ppermute | solution.py:51
  535.1 48.4 %collective-permute-start.1 = (bf16[8]{0:T(256)(128)(2,1)S(1)}, bf16[8]{0:T(256)(128)(2,1)S(1)}, u32[]{:S(2)}, u32[]{:S(2)}) collective-permute-start(bf16[8]{0:T(256)(128)(2,1)S(1)} %get-tuple-element.95), channel_id=1, source_target_pairs={{8,0},{12,4},{16,8},{20,12},{24,16},{28,20},{9,1},{13,5},{17,9},{2... | collective-permute-start | bytes 56 | tf_op jit(solution)/shard_map/ppermute | solution.py:51
  584.0 93.3 %collective-permute-start.6 = (bf16[8,131072]{1,0:T(8,128)(2,1)S(1)}, bf16[8,131072]{1,0:T(8,128)(2,1)S(1)}, u32[]{:S(2)}, u32[]{:S(2)}) collective-permute-start(bf16[8,131072]{1,0:T(8,128)(2,1)S(1)} %get-tuple-element.93), channel_id=1, source_target_pairs={{16,0},{20,4},{24,8},{28,12},{17,1},{21,5},{25,9},{29,13},{18,2},{... | collective-permute-start | bytes 6291464 | tf_op jit(solution)/shard_map/ppermute | solution.py:51
  (10 other events, 20.5 us)
Sparse Core Ops, SparseCore 0:
  68.0 311.7 all-reduce.2
where the time goes:
time: 696 us; the launch traced here: 687 us
  blocking collectives  281 us (40%)
  waiting for transfers between devices  180 us (26%)
  local copies, waits for them, and re-layouts  71.1 us (10%)
  matrix products  62.4 us (9%)
  other arithmetic  42.4 us (6%)
  starting transfers between devices  32 us (5%)
  between operations  14.3 us (2%)
    unnamed x1, blocking collectives  281 us
    ppermute x5, waiting for transfers between devices, shifted(): return lax.ppermute(x, axis, pairs)  180 us
    dot_general x8, matrix products, tile_stats(): jnp.einsum(spec_out, weights, value_tile, preferred_element_type=jnp.floa...  39.4 us
    unnamed x63, local copies, waits for them, and re-layouts  23.7 us
    dot_general x8, matrix products, tile_stats(): jnp.einsum(spec_scores, query_blocks, key_tile, preferred_element_type=jn...  21.5 us
    gather x1, local copies, waits for them, and re-layouts, body(): replies[holders, head_rows, rank].reshape(head_dev, blk_dev, R, 2, B, DH)  14.2 us
    reduce_sum x4, other arithmetic, tile_stats(): row_sum = jnp.sum(weights, axis=-1, dtype=jnp.float32)  14 us
  transfers between devices with their start and end apart: 10, of which 3 were waited for; matrix products, arithmetic and copies ran while one was open for 9% of the time, Pallas kernels for 0%

commit v1 on v0

v1 whole, which is shorter than its diff:
```python
import functools
import math

import jax
import jax.numpy as jnp
from jax import lax
from jax.experimental import pallas as pl
from jax.experimental.pallas import tpu as pltpu
from jax.sharding import PartitionSpec as P

DH = 128
B = 128
G = 2
R = 3

neg_big = -1e30
ANYWHERE = pltpu.CompilerParams(
    dimension_semantics=("arbitrary",), vmem_limit_bytes=60 * 1024 * 1024
)


def halo(block, axis, width):
    count = lax.axis_size(axis)
    forward = [(i, i + 1) for i in range(count - 1)]
    backward = [(target, source) for source, target in forward]
    low = lax.ppermute(block[-width:], axis, forward)
    high = lax.ppermute(block[:width], axis, backward)
    return jnp.concatenate([low, high], axis=0)


def broadcast(block, axis, source):
    block = jnp.where(lax.axis_index(axis) == source, block, jnp.zeros_like(block))
    return lax.psum(block, axis)


def pick_kernel(cap, head_ref, block_ref, k_ref, v_ref, out_ref):
    dest = pl.program_id(0)

    @pl.loop(0, cap)
    def _(j):
        rows = pl.ds(pl.multiple_of(block_ref[dest, j] * B, B), B)
        cols = pl.ds(pl.multiple_of(head_ref[dest, j] * DH, DH), DH)
        out_ref[j, 0] = k_ref[rows, cols]
        out_ref[j, 1] = v_ref[rows, cols]


def pick(keys, values, heads, blocks, seq_count, cap):
    whole = pl.BlockSpec(keys.shape, lambda d, *_: (0, 0))
    return pl.pallas_call(
        functools.partial(pick_kernel, cap),
        out_shape=jax.ShapeDtypeStruct((seq_count * cap, 2, B, DH), keys.dtype),
        grid_spec=pltpu.PrefetchScalarGridSpec(
            num_scalar_prefetch=2,
            grid=(seq_count,),
            in_specs=[whole, whole],
            out_specs=pl.BlockSpec((cap, 2, B, DH), lambda d, *_: (d, 0, 0, 0)),
        ),
        compiler_params=ANYWHERE,
    )(heads, blocks, keys, values)


def attend_kernel(
    blk_dev,
    keep_ref,
    slot_ref,
    live_ref,
    where_ref,
    q_ref,
    k_ref,
    v_ref,
    hk_ref,
    hv_ref,
    gk_ref,
    gv_ref,
    rand_ref,
    out_ref,
):
    scale = 1.0 / math.sqrt(DH)
    head = pl.program_id(0)
    out_ref[...] = jnp.zeros_like(out_ref)

    def tile(ref, halo_ref, i):
        if i < 0:
            return halo_ref[:B]
        if i >= blk_dev:
            return halo_ref[B:]
        return ref[i * B : (i + 1) * B]

    def one(i):
        q = q_ref[i * B : (i + 1) * B]
        near = range(i - 1, i + 2)
        picks = [where_ref[(head * blk_dev + i) * R + r] for r in range(R)]
        k_parts = [
            jnp.concatenate([tile(k_ref, hk_ref, n) for n in near], axis=0),
            gk_ref[...],
            jnp.concatenate([rand_ref[p, 0] for p in picks], axis=0),
        ]
        v_parts = [
            jnp.concatenate([tile(v_ref, hv_ref, n) for n in near], axis=0),
            gv_ref[...],
            jnp.concatenate([rand_ref[p, 1] for p in picks], axis=0),
        ]
        scores = [
            lax.dot_general(
                q, k, (((1,), (1,)), ((), ())), preferred_element_type=jnp.float32
            )
            * scale
            for k in k_parts
        ]
        lanes = lax.broadcasted_iota(jnp.int32, scores[0].shape, 1)
        if i == 0:
            dead = jnp.logical_and(lanes < B, live_ref[0] == 0)
            scores[0] = jnp.where(dead, neg_big, scores[0])
        if i == blk_dev - 1:
            dead = jnp.logical_and(lanes >= 2 * B, live_ref[1] == 0)
            scores[0] = jnp.where(dead, neg_big, scores[0])
        peak = functools.reduce(
            jnp.maximum, [jnp.max(s, axis=-1, keepdims=True) for s in scores]
        )
        numer = jnp.zeros((B, DH), jnp.float32)
        denom = jnp.zeros((B, 1), jnp.float32)
        for s, v in zip(scores, v_parts):
            w = jnp.exp(s - peak).astype(jnp.bfloat16)
            denom = denom + jnp.sum(w.astype(jnp.float32), axis=-1, keepdims=True)
            numer = numer + jnp.dot(w, v, preferred_element_type=jnp.float32)
        rows = pl.ds(pl.multiple_of(slot_ref[i] * B, B), B)
        out_ref[rows, :] = (numer / denom).astype(out_ref.dtype)

    for i in range(blk_dev):
        pl.when(keep_ref[i] > 0)(functools.partial(one, i))


def attend(keep, slot, live, where, q, k, v, hk, hv, gk, gv, rand):
    tok_dev, width_dev = q.shape
    blk_dev, head_dev = tok_dev // B, width_dev // DH

    def column(rows):
        return pl.BlockSpec((rows, DH), lambda h, *_: (0, h))

    return pl.pallas_call(
        functools.partial(attend_kernel, blk_dev),
        out_shape=jax.ShapeDtypeStruct(q.shape, q.dtype),
        grid_spec=pltpu.PrefetchScalarGridSpec(
            num_scalar_prefetch=4,
            grid=(head_dev,),
            in_specs=[column(tok_dev)] * 3
            + [column(2 * B)] * 2
            + [column(G * B)] * 2
            + [pl.BlockSpec(rand.shape, lambda h, *_: (0, 0, 0, 0))],
            out_specs=column(tok_dev),
        ),
        compiler_params=ANYWHERE,
    )(keep, slot, live, where, q, k, v, hk, hv, gk, gv, rand)


def copy_kernel(order_ref, in_ref, out_ref):
    out_ref[...] = in_ref[...]


def take_blocks(blocks, order, cap):
    width = blocks.shape[1]
    return pl.pallas_call(
        copy_kernel,
        out_shape=jax.ShapeDtypeStruct((cap * B, width), blocks.dtype),
        grid_spec=pltpu.PrefetchScalarGridSpec(
            num_scalar_prefetch=1,
            grid=(cap,),
            in_specs=[pl.BlockSpec((B, width), lambda j, order: (order[j], 0))],
            out_specs=pl.BlockSpec((B, width), lambda j, order: (j, 0)),
        ),
        compiler_params=ANYWHERE,
    )(order, blocks)


def merge_kernel(kind_ref, from_ref, old_ref, new_ref, out_ref):
    kind = kind_ref[pl.program_id(0)]

    @pl.when(kind == 0)
    def _():
        out_ref[...] = old_ref[...]

    @pl.when(kind == 1)
    def _():
        out_ref[...] = jnp.zeros_like(out_ref)

    @pl.when(kind == 2)
    def _():
        out_ref[...] = new_ref[...]


def merge_blocks(old, new, kind, place):
    tok_dev, width = old.shape
    return pl.pallas_call(
        merge_kernel,
        out_shape=jax.ShapeDtypeStruct(old.shape, old.dtype),
        grid_spec=pltpu.PrefetchScalarGridSpec(
            num_scalar_prefetch=2,
            grid=(tok_dev // B,),
            in_specs=[
                pl.BlockSpec((B, width), lambda j, kind, place: (j, 0)),
                pl.BlockSpec((B, width), lambda j, kind, place: (place[j], 0)),
            ],
            out_specs=pl.BlockSpec((B, width), lambda j, kind, place: (j, 0)),
        ),
        compiler_params=ANYWHERE,
    )(kind, place, old, new)


def exclusive(flags, axis):
    return jnp.cumsum(flags, axis=axis) - flags


def first_at_least(caps, amount):
    return jnp.sum((amount > jnp.asarray(caps, jnp.int32)).astype(jnp.int32))


def body(queries, keys, values, random_holder, random_offset, keep):
    tok_dev, width_dev = queries.shape
    blk_dev = tok_dev // B
    head_dev = width_dev // DH
    seq_count = lax.axis_size("seq")
    head_count = lax.axis_size("head")
    me = lax.axis_index("seq")
    count_req = blk_dev * R
    total = head_dev * count_req
    i32 = jnp.int32

    code = random_holder * blk_dev + random_offset
    code = jnp.where((keep > 0)[None, :, None], code, -1).reshape(total)
    table = lax.all_gather(jnp.concatenate([code, keep]), ("seq", "head"))
    table = table.reshape(seq_count, head_count, total + blk_dev)
    keep_all = table[:, 0, total:].reshape(seq_count * blk_dev)
    codes = table[:, :, :total]
    devices = jnp.arange(seq_count, dtype=i32)

    halo_k, halo_v = halo(keys, "seq", B), halo(values, "seq", B)
    glob_k, glob_v = broadcast(jnp.stack((keys[: G * B], values[: G * B])), "seq", 0)

    named = jnp.where(codes >= 0, codes // blk_dev, -1)
    counts = jnp.sum((named[..., None] == devices).astype(i32), axis=2)
    most = jnp.max(counts)
    onehot = (named[me, lax.axis_index("head")][:, None] == devices).astype(i32)
    mine = exclusive(onehot, 0)
    my_slot = jnp.sum(mine * onehot, axis=1)
    my_holder = jnp.sum(onehot * devices, axis=1)

    group = codes[:, lax.axis_index("head")]
    asks = (named[:, lax.axis_index("head")] == me).astype(i32)
    order = exclusive(asks, 1)
    full = min(total, head_dev * max(2, (count_req + seq_count - 1) // seq_count))
    chosen = asks[..., None] * (order[..., None] == jnp.arange(full, dtype=i32)).astype(i32)
    ask_head = jnp.arange(total, dtype=i32) // count_req
    ask = jnp.where(group >= 0, group % blk_dev, 0) + ask_head[None] * blk_dev
    ask = jnp.sum(chosen * ask[..., None], axis=1)
    pick_head, pick_block = ask // blk_dev, ask % blk_dev

    rank = exclusive(keep_all, 0)
    slot = rank % blk_dev
    source = jnp.arange(seq_count * blk_dev, dtype=i32) // blk_dev
    distance = jnp.where(keep_all > 0, source - rank // blk_dev, 0)
    my_slots = lax.dynamic_slice_in_dim(slot, me * blk_dev, blk_dev)
    live = jnp.stack([me > 0, me < seq_count - 1]).astype(i32)

    caps = sorted({max(1, full * part // 12) for part in range(5, 13)})

    def gathered(cap):
        def run(q, k, v, hk, hv, gk, gv):
            picked = pick(k, v, pick_head, pick_block, seq_count, cap)
            replies = lax.all_to_all(picked, "seq", split_axis=0, concat_axis=0, tiled=True)
            where = jnp.minimum(my_holder * cap + my_slot, seq_count * cap - 1)
            return attend(keep, my_slots, live, where, q, k, v, hk, hv, gk, gv, replies)

        return run

    blocks = lax.switch(
        first_at_least(caps[:-1], most),
        [gathered(cap) for cap in caps],
        queries, keys, values, halo_k, halo_v, glob_k, glob_v,
    )

    slots = jnp.arange(blk_dev, dtype=i32)
    sizes = sorted({0, *range(blk_dev // 2 - 1, blk_dev + 1)})
    for bit_pos in range((seq_count - 1).bit_length()):
        stride = 2**bit_pos
        at = source - distance % stride
        moving = (keep_all > 0) & (distance // stride % 2 > 0)
        on_slot = ((slot[:, None] == slots) & moving[:, None]).astype(i32)
        on_device = (at[:, None] == devices).astype(i32)
        leaving = jnp.sum(on_device[:, :, None] * on_slot[:, None, :], axis=0)
        needed = jnp.max(jnp.sum(leaving, axis=1))
        nth = exclusive(leaving, 1)
        mine_out, mine_nth = leaving[me], nth[me]
        send = jnp.sum(
            mine_out[:, None] * (mine_nth[:, None] == slots).astype(i32) * slots[:, None], axis=0
        )
        far = jnp.minimum(me + stride, seq_count - 1)
        comes = jnp.where(me + stride < seq_count, leaving[far], 0)
        kind = jnp.where(comes > 0, 2, jnp.where(mine_out > 0, 1, 0)).astype(i32)
        place = jnp.where(comes > 0, nth[far], 0)
        all_pairs = [(i, i - stride) for i in range(stride, seq_count)]
        split = seq_count - stride // 2
        upper = [pair for pair in all_pairs if pair[0] >= split]
        halves = 2 * stride >= seq_count and 0 < len(upper) < len(all_pairs)

        def shifting(cap, pairs, send=send, kind=kind, place=place):
            def run(blocks):
                if cap == 0:
                    return blocks
                moved = lax.ppermute(take_blocks(blocks, send, cap), "seq", pairs)
                return merge_blocks(blocks, moved, kind, jnp.minimum(place, cap - 1))

            return run

        which = first_at_least(sizes[:-1], needed)
        runs = [shifting(cap, all_pairs) for cap in sizes]
        if halves:
            runs += [shifting(cap, upper) for cap in sizes]
            lower = jnp.sum(leaving * (devices < split)[:, None].astype(i32))
            which = which + jnp.where(lower > 0, 0, len(sizes))
        blocks = lax.switch(which, runs, blocks)
    return blocks


def solution(mesh):
    in_specs = (
        P("seq", "head"),
        P("seq", "head"),
        P("seq", "head"),
        P("head", "seq", None),
        P("head", "seq", None),
        P("seq"),
    )
    out_specs = P("seq", "head")
    return jax.shard_map(body, mesh=mesh, in_specs=in_specs, out_specs=out_specs, check_vma=False)
```

time: 696 us -> 566 us (0.81)
  the two profiles are of different devices: /device:TPU:2 before, /device:TPU:10 now
where the time goes in v1:
time: 566 us; the launch traced here: 565 us
  waiting for transfers between devices  352 us (62%)
  Pallas kernels  61.8 us (11%)
  blocking collectives  52.3 us (9%)
  starting transfers between devices  29.1 us (5%)
  other arithmetic  20.4 us (4%)
  between operations  17.3 us (3%)
  local copies, waits for them, and re-layouts  16.2 us (3%)
  loops' own time  15.8 us (3%)
    all_to_all x1, waiting for transfers between devices, run(): lax.all_to_all(picked, 'seq', split_axis=0, concat_axis=0, tiled=True)  247 us
    ppermute x3, waiting for transfers between devices, run(): moved = lax.ppermute(take_blocks(blocks, send, cap), 'seq', pairs)  98.1 us
    unnamed x1, blocking collectives  52.3 us
    pallas_call x1, Pallas kernels, attend(): pl.pallas_call(functools.partial(attend_kernel, blk_dev), out_shape=jax.S...  25 us
    another operation x1, loops' own time, body(): lax.switch(first_at_least(caps[:-1], most), [gathered(cap) for cap in cap...  15.6 us
    pallas_call x3, Pallas kernels, merge_blocks(): pl.pallas_call(merge_kernel, out_shape=jax.ShapeDtypeStruct(old.shape, ol...  14.9 us
    pallas_call x3, Pallas kernels, take_blocks(): pl.pallas_call(copy_kernel, out_shape=jax.ShapeDtypeStruct((cap * B, widt...  12.2 us
  transfers between devices with their start and end apart: 9, of which 5 were waited for; matrix products, arithmetic and copies ran while one was open for 3% of the time, Pallas kernels for 0%

profile of v1, /device:TPU:10, one launch (start us, length us, event | category | flops | bytes accessed | tf_op | source)
XLA Modules:
  0.0 564.6 jit_solution(700056085134987355)
XLA Ops:
  10.9 3.5 collective-permute-start.26
  17.7 4.3 collective-permute-start.24
  24.5 52.3 %all-reduce.2 = s32[6400]{0:T(1024)S(1)} all-reduce(s32[6400]{0:T(1024)S(1)} %add_dynamic-update-slice_fusion), channel_id=2, replica_groups=mesh['seq'=8,'head'=4] {'seq','head'}, use_global_device_ids=true, to_apply=%add.2 | all-reduce | flops 6400 | bytes 51200
  84.2 2.6 fusion.144
  95.4 6.8 %all-reduce.5.cloned.1.call-done = bf16[2,256,1024]{2,1,0:T(8,128)(2,1)} async-done(((bf16[2,256,1024]{2,1,0:T(8,128)(2,1)}), bf16[2,256,1024]{2,1,0:T(8,128)(2,1)}) %all-reduce.5.cloned.1.call-update) | async-done | bytes 1048592 | tf_op jit(solution)/shard_map/psum | solution.py:33
  104.5 303.9 %conditional.4 = (bf16[1024,1024]{1,0:T(8,128)(2,1)S(1)}) conditional(s32[]{:T(128)} %clamp.15, (s32[192]{0:T(256)S(1)}, s32[192]{0:T(256)S(1)}, s32[8,24]{1,0:T(8,128)S(1)}, s32[8,24]{1,0:T(8,128)S(1)}, bf16[1024,1024]{1,0:T(8,128)(2,1)S(1)}, /*index=5*/bf16[1024,1024]{1,0:T(8,128)(2,1)}, s32[8]{0:T(128)S(1)}, ...), branch_computations={%region_23.24_spmd, %region_24.25_spmd, %region_25.26_spmd, %regio... | conditional | flops 576 | bytes 46139716 | solution.py:275
  112.8 9.6 %branch_6_fun.8 = bf16[176,2,128,128]{3,2,1,0:T(8,128)(2,1)} custom-call(s32[8,24]{1,0:T(8,128)S(1)} %get-tuple-element.1341.head_ref, s32[8,24]{1,0:T(8,128)S(1)} %get-tuple-element.1342.block_ref, bf16[1024,1024]{1,0:T(8,128)(2,1)S(1)} %get-tuple-element.1335.k_ref, bf16[1024,1024]{1,0:T(8,128)(2,1)} %get-tuple-element.1336.v_ref), custom_call_target="tpu_custom_call" | custom-call | tf_op jit(solution)/shard_map/cond/branch_6_fun/pallas_call | solution.py:49
  122.4 6.2 %all-to-all-start.6 = ((bf16[176,2,128,128]{3,2,1,0:T(8,128)(2,1)}), bf16[176,2,128,128]{3,2,1,0:T(8,128)(2,1)}, u32[]{:S(2)}, u32[]{:S(2)}) async-start(bf16[176,2,128,128]{3,2,1,0:T(8,128)(2,1)} %branch_6_fun.8), calls=%async_computation.6 | async-start | bytes 23068672 | tf_op jit(solution)/shard_map/cond/branch_6_fun/all_to_all | solution.py:269
  129.2 246.8 %all-to-all-done.6.rand_ref = bf16[176,2,128,128]{3,2,1,0:T(8,128)(2,1)} async-done(((bf16[176,2,128,128]{3,2,1,0:T(8,128)(2,1)}), bf16[176,2,128,128]{3,2,1,0:T(8,128)(2,1)}, u32[]{:S(2)}, u32[]{:S(2)}) %all-to-all-start.6) | async-done | bytes 11534368 | tf_op jit(solution)/shard_map/cond/branch_6_fun/all_to_all | solution.py:269
  376.0 25.0 %branch_6_fun.9 = bf16[1024,1024]{1,0:T(8,128)(2,1)S(1)} custom-call(s32[8]{0:T(128)S(1)} %get-tuple-element.1329.keep_ref, s32[8]{0:T(128)S(1)} %get-tuple-element.1330.slot_ref, s32[2]{0:T(128)S(1)} %get-tuple-element.1331.live_ref, s32[192]{0:T(256)} %add_minimum_fusion.6.where_ref, bf16[1024,1024]{1,0:T(8,128)(2,1)} %get-tuple-element.1334.q_ref, ...), custom_call_target="tpu_custom_call" | custom-call | tf_op jit(solution)/shard_map/cond/branch_6_fun/pallas_call | solution.py:140
  408.5 46.0 %conditional.5 = (bf16[1024,1024]{1,0:T(8,128)(2,1)S(1)}) conditional(s32[]{:T(128)} %clamp.14, bf16[1024,1024]{1,0:T(8,128)(2,1)S(1)} %get-tuple-element.2286, (s32[]{:T(128)}, s32[8,8]{1,0:T(8,128)S(1)}, bf16[1024,1024]{1,0:T(8,128)(2,1)S(1)}, (), s32[8,8]{1,0:T(8,128)S(1)}, /*index=5*/s32[8]{0:T(128)S(1)}, ...), branch_computations={%region_34.35_spmd, %region_35.36_spmd, %region_36.37_spmd, %regio... | conditional | flops 369 | bytes 20973610 | solution.py:320
  411.1 3.8 branch_3_fun.10
  414.9 4.1 collective-permute-start.15
  419.1 29.6 %collective-permute-done.15.new_ref = bf16[640,1024]{1,0:T(8,128)(2,1)S(1)} collective-permute-done((bf16[640,1024]{1,0:T(8,128)(2,1)}, bf16[640,1024]{1,0:T(8,128)(2,1)S(1)}, u32[]{:S(2)}, u32[]{:S(2)}) %collective-permute-start.15) | collective-permute-done | bytes 1310752 | tf_op jit(solution)/shard_map/cond/branch_3_fun/ppermute | solution.py:309
  449.7 4.9 branch_3_fun.11
  454.6 68.3 %conditional.6 = (bf16[1024,1024]{1,0:T(8,128)(2,1)S(1)}) conditional(s32[]{:T(128)} %clamp.13, bf16[1024,1024]{1,0:T(8,128)(2,1)S(1)} %get-tuple-element.2287, (s32[]{:T(128)}, s32[8,8]{1,0:T(8,128)S(1)}, bf16[1024,1024]{1,0:T(8,128)(2,1)S(1)}, (), s32[8,8]{1,0:T(8,128)S(1)}, /*index=5*/s32[8]{0:T(128)S(1)}, ...), branch_computations={%region_44.45_spmd, %region_45.46_spmd, %region_46.47_spmd, %regio... | conditional | flops 369 | bytes 20973610 | solution.py:320
  457.2 5.4 branch_5_fun.12
  462.6 5.3 collective-permute-start.22
  467.9 48.6 %collective-permute-done.22.new_ref = bf16[896,1024]{1,0:T(8,128)(2,1)S(1)} collective-permute-done((bf16[896,1024]{1,0:T(8,128)(2,1)}, bf16[896,1024]{1,0:T(8,128)(2,1)S(1)}, u32[]{:S(2)}, u32[]{:S(2)}) %collective-permute-start.22) | collective-permute-done | bytes 1835040 | tf_op jit(solution)/shard_map/cond/branch_5_fun/ppermute | solution.py:309
  517.8 5.1 branch_5_fun.13
  522.9 33.3 %conditional.7 = (bf16[1024,1024]{1,0:T(8,128)(2,1)S(1)}) conditional(s32[]{:T(128)} %clamp.12, bf16[1024,1024]{1,0:T(8,128)(2,1)S(1)} %get-tuple-element.2288, (s32[]{:T(128)}, s32[8,8]{1,0:T(8,128)S(1)}, s32[8]{0:T(128)S(1)}, s32[]{:T(128)}, s32[8]{0:T(128)S(1)}, /*index=5*/s32[8]{0:T(128)S(1)}, ...), branch_computations={%region_52.53_spmd, %region_53.55_spmd, %region_55.57_spmd, %regio... | conditional | flops 382 | bytes 20973724 | solution.py:320
  526.0 3.1 branch_8_fun.2
  530.3 20.0 %collective-permute-done.8.new_ref = bf16[384,1024]{1,0:T(8,128)(2,1)S(1)} collective-permute-done((bf16[384,1024]{1,0:T(8,128)(2,1)}, bf16[384,1024]{1,0:T(8,128)(2,1)S(1)}, u32[]{:S(2)}, u32[]{:S(2)}) %collective-permute-start.8) | collective-permute-done | bytes 786464 | tf_op jit(solution)/shard_map/cond/branch_8_fun/ppermute | solution.py:309
  551.2 5.0 branch_8_fun.3
  (129 shorter events, 39.6 us)
Async XLA Ops:
  6.5 95.7 %all-reduce.5.cloned.1.call-start = ((), (), s32[]{:S(2)}) async-start(), calls=%async_computation.8 | async-start | bytes 2097152 | tf_op jit(solution)/shard_map/psum | solution.py:33
  8.7 8.1 %copy-start.1 = (bf16[1024,1024]{1,0:T(8,128)(2,1)S(1)}, bf16[1024,1024]{1,0:T(8,128)(2,1)}, u32[]{:S(2)}) copy-start(bf16[1024,1024]{1,0:T(8,128)(2,1)} %param.47) | copy-start | bytes 6291460
  9.8 14.2 %copy-start.37 = (s32[8]{0:T(128)S(1)}, s32[8]{0:T(128)}, u32[]{:S(2)}) copy-start(s32[8]{0:T(128)} %param.51) | copy-start | bytes 100
  9.8 14.2 %copy-start.38 = (s32[8,8,3]{1,0,2:T(8,128)S(1)}, s32[8,8,3]{1,0,2:T(8,128)}, u32[]{:S(2)}) copy-start(s32[8,8,3]{1,0,2:T(8,128)} %param.50) | copy-start | bytes 2308
  9.8 14.2 %copy-start.39 = (s32[8,8,3]{1,0,2:T(8,128)S(1)}, s32[8,8,3]{1,0,2:T(8,128)}, u32[]{:S(2)}) copy-start(s32[8,8,3]{1,0,2:T(8,128)} %param.49) | copy-start | bytes 2308
  9.8 74.4 %copy-start.40 = (s32[6]{0:T(128)S(1)}, s32[6]{0:T(128)}, u32[]{:S(2)}) copy-start(s32[6]{0:T(128)} %constant.391.clone) | copy-start | bytes 76
  9.8 77.8 %copy-start.41 = (s32[7]{0:T(128)S(1)}, s32[7]{0:T(128)}, u32[]{:S(2)}) copy-start(s32[7]{0:T(128)} %constant.390.clone) | copy-start | bytes 88
  10.9 82.3 %collective-permute-start.26 = (bf16[128,1024]{1,0:T(8,128)(2,1)S(1)}, bf16[128,1024]{1,0:T(8,128)(2,1)S(1)}, u32[]{:S(2)}, u32[]{:S(2)}) collective-permute-start(bf16[128,1024]{1,0:T(8,128)(2,1)S(1)} %get-tuple-element.2248), channel_id=1, source_target_pairs={{0,4},{4,8},{8,12},{12,16},{16,20},{20,24},{24,28},{1,5},{5,9},{9,... | collective-permute-start | bytes 786440 | tf_op jit(solution)/shard_map/ppermute | solution.py:26
  14.4 78.9 %collective-permute-start.27 = (bf16[128,1024]{1,0:T(8,128)(2,1)S(1)}, bf16[128,1024]{1,0:T(8,128)(2,1)}, u32[]{:S(2)}, u32[]{:S(2)}) collective-permute-start(bf16[128,1024]{1,0:T(8,128)(2,1)S(1)} %get-tuple-element.2249), channel_id=1, source_target_pairs={{4,0},{8,4},{12,8},{16,12},{20,16},{24,20},{28,24},{5,1},{9,5},{13... | collective-permute-start | bytes 786440 | tf_op jit(solution)/shard_map/ppermute | solution.py:27
  17.7 76.6 %collective-permute-start.24 = (bf16[128,1024]{1,0:T(8,128)(2,1)}, bf16[128,1024]{1,0:T(8,128)(2,1)}, u32[]{:S(2)}, u32[]{:S(2)}) collective-permute-start(bf16[128,1024]{1,0:T(8,128)(2,1)} %get-tuple-element.2250), channel_id=1, source_target_pairs={{0,4},{4,8},{8,12},{12,16},{16,20},{20,24},{24,28},{1,5},{5,9},{9,... | collective-permute-start | bytes 786440 | tf_op jit(solution)/shard_map/ppermute | solution.py:26
  22.0 72.3 %collective-permute-start.25 = (bf16[128,1024]{1,0:T(8,128)(2,1)}, bf16[128,1024]{1,0:T(8,128)(2,1)}, u32[]{:S(2)}, u32[]{:S(2)}) collective-permute-start(bf16[128,1024]{1,0:T(8,128)(2,1)} %get-tuple-element.2251), channel_id=1, source_target_pairs={{4,0},{8,4},{12,8},{16,12},{20,16},{24,20},{28,24},{5,1},{9,5},{13... | collective-permute-start | bytes 786440 | tf_op jit(solution)/shard_map/ppermute | solution.py:27
  81.5 11.8 %copy-start.22 = (s32[8,8]{1,0:T(8,128)}, s32[8,8]{1,0:T(8,128)S(1)}, u32[]{:S(2)}) copy-start(s32[8,8]{1,0:T(8,128)S(1)} %get-tuple-element.2154) | copy-start | bytes 772
  112.8 9.7 %copy-start.8 = (bf16[1024,1024]{1,0:T(8,128)(2,1)}, bf16[1024,1024]{1,0:T(8,128)(2,1)S(1)}, u32[]{:S(2)}) copy-start(bf16[1024,1024]{1,0:T(8,128)(2,1)S(1)} %get-tuple-element.1335.k_ref) | copy-start | bytes 6291460 | tf_op jit(solution)/shard_map/cond
  122.4 253.6 %all-to-all-start.6 = ((bf16[176,2,128,128]{3,2,1,0:T(8,128)(2,1)}), bf16[176,2,128,128]{3,2,1,0:T(8,128)(2,1)}, u32[]{:S(2)}, u32[]{:S(2)}) async-start(bf16[176,2,128,128]{3,2,1,0:T(8,128)(2,1)} %branch_6_fun.8), calls=%async_computation.6 | async-start | bytes 23068672 | tf_op jit(solution)/shard_map/cond/branch_6_fun/all_to_all | solution.py:269
  414.9 33.7 %collective-permute-start.15 = (bf16[640,1024]{1,0:T(8,128)(2,1)}, bf16[640,1024]{1,0:T(8,128)(2,1)S(1)}, u32[]{:S(2)}, u32[]{:S(2)}) collective-permute-start(bf16[640,1024]{1,0:T(8,128)(2,1)} %branch_3_fun.10), channel_id=1, source_target_pairs={{4,0},{8,4},{12,8},{16,12},{20,16},{24,20},{28,24},{5,1},{9,5},{13... | collective-permute-start | bytes 3932168 | tf_op jit(solution)/shard_map/cond/branch_3_fun/ppermute | solution.py:309
  448.6 1.1 copy-start.26
  454.6 68.3 %copy-start.23 = (s32[8,8]{1,0:T(8,128)S(1)}, s32[8,8]{1,0:T(8,128)}, u32[]{:S(2)}) copy-start(s32[8,8]{1,0:T(8,128)} %copy-done.22) | copy-start | bytes 772
  454.6 68.3 %copy-start.36 = (s32[8,8]{1,0:T(8,128)S(1)}, s32[8,8]{1,0:T(8,128)}, u32[]{:S(2)}) copy-start(s32[8,8]{1,0:T(8,128)} %reduce_window_sum.66) | copy-start | bytes 772
  462.6 53.9 %collective-permute-start.22 = (bf16[896,1024]{1,0:T(8,128)(2,1)}, bf16[896,1024]{1,0:T(8,128)(2,1)S(1)}, u32[]{:S(2)}, u32[]{:S(2)}) collective-permute-start(bf16[896,1024]{1,0:T(8,128)(2,1)} %branch_5_fun.12), channel_id=1, source_target_pairs={{8,0},{12,4},{16,8},{20,12},{24,16},{28,20},{9,1},{13,5},{17,9},{2... | collective-permute-start | bytes 5505032 | tf_op jit(solution)/shard_map/cond/branch_5_fun/ppermute | solution.py:309
  516.5 1.3 copy-start.17
  529.0 21.3 %collective-permute-start.8 = (bf16[384,1024]{1,0:T(8,128)(2,1)}, bf16[384,1024]{1,0:T(8,128)(2,1)S(1)}, u32[]{:S(2)}, u32[]{:S(2)}) collective-permute-start(bf16[384,1024]{1,0:T(8,128)(2,1)} %branch_8_fun.2), channel_id=1, source_target_pairs={{24,8},{28,12},{25,9},{29,13},{26,10},{30,14},{27,11},{31,15}} | collective-permute-start | bytes 2359304 | tf_op jit(solution)/shard_map/cond/branch_8_fun/ppermute | solution.py:309
  550.3 0.9 copy-start.33
  556.2 1.3 copy-start
Sparse Core Ops, SparseCore 0:
  10.8 91.3 all-reduce.4
